TPU v7x, 32 devices: a whole 2x2x4 slice. The times are simulated.
32 devices in a mesh: section: 2 (over x), dp: 16 (over z, y, core).
Axes of the slice: x: 2, y: 2, z: 4, core: 2. Of those that a mesh axis runs over, the one named last changes fastest.
Arguments:
- features: bfloat16 [1, 2, 2048, 4096], P(None, 'section', 'dp'), parts along dimension 2, may hold values from -6 to 6
- in_proj: bfloat16 [2, 4096, 512], P('section'), may hold values from -0.09375 to 0.09375
- mix_proj: bfloat16 [2, 2, 256, 256], P('section'), may hold values from -0.375 to 0.375
- out_proj: bfloat16 [2, 512, 4096], P('section'), may hold values from -0.375 to 0.375
- gate_proj: bfloat16 [2, 2, 4096], P('section'), may hold values from -0.09375 to 0.09375
- cross_bias: float32 [2, 4096], P('section'), may hold values from -3 to 3
Outputs:
- crossed: bfloat16 [1, 2, 2048, 4096], P(None, 'section', 'dp'), parts along dimension 2
There are 16 independent parts, one for each index of `dp`. A program takes and returns all parts, laid end to end along the dimension named above; an argument that names none is the same for every part. Nothing has to cross between parts.
All inputs are finite; a program needn't handle non-finite values.
Results may differ from a plain program's by a relative error of at most 0.015.
Values may be sent and summed in bfloat16 or wider, within the bound.
No kernel may reach another device: no remote copies, remote signals or barrier semaphores. Data moves between devices by JAX's collectives and lax.ppermute only.
A program may use at most 64 MiB of HBM per device.

v0:
```python
import jax
import jax.numpy as jnp
from jax import lax
from jax.sharding import PartitionSpec as P


def from_behind(block, axis, distance):
    devices = range(lax.axis_size(axis))
    route = [(i - distance, i) for i in devices if i - distance in devices]
    return lax.ppermute(block, axis, route)


def cross_layer(current, anchor, v_mat, c_mat, u_mat, gate_mat, shift_row):
    row_count = current.shape[0]
    expert_count = c_mat.shape[0]
    rank_size = c_mat.shape[1]
    projected = jnp.dot(current, v_mat, preferred_element_type=jnp.float32)
    inner_first = (
        jnp.tanh(projected).astype(jnp.bfloat16).reshape(row_count, expert_count, rank_size)
    )
    inner_second = jnp.einsum(
        "rek,ekj->rej", inner_first, c_mat, preferred_element_type=jnp.float32
    )
    logits = lax.dot_general(
        current, gate_mat, (((1,), (1,)), ((), ())), preferred_element_type=jnp.float32
    )
    gate_values = 1.0 / jnp.sum(jnp.exp(logits[:, None, :] - logits[:, :, None]), axis=2)
    blended = (gate_values[:, :, None] * jnp.tanh(inner_second)).astype(jnp.bfloat16)
    blended = blended.reshape(row_count, expert_count * rank_size)
    crossed = jnp.dot(blended, u_mat, preferred_element_type=jnp.float32)
    updated = current.astype(jnp.float32) + anchor.astype(jnp.float32) * (crossed + shift_row)
    return updated.astype(jnp.bfloat16)


def per_device(features, in_proj, mix_proj, out_proj, gate_proj, cross_bias):
    section_count = lax.axis_size("section")
    position = lax.axis_index("section")
    pieces = 1
    local_micro = features.shape[0]
    row_count = features.shape[2]
    feature_count = features.shape[3]
    piece_rows = row_count // pieces
    everyone = lax.all_gather(features, "section", axis=1, tiled=True)
    all_units = everyone.reshape(local_micro * section_count * pieces, piece_rows, feature_count)
    unit_count = all_units.shape[0]
    step_count = unit_count + section_count - 1
    v_mat = in_proj[0]
    c_mat = mix_proj[0]
    u_mat = out_proj[0]
    gate_mat = gate_proj[0]
    shift_row = cross_bias[0]

    def apply_layer(current, anchor):
        return cross_layer(current, anchor, v_mat, c_mat, u_mat, gate_mat, shift_row)

    def keep_input(current, anchor):
        return current

    def advance(carried, moment):
        incoming, outgoing, collected = carried
        unit_here = moment - position
        active = (unit_here >= 0) & (unit_here < unit_count)
        anchor = lax.dynamic_index_in_dim(
            all_units, jnp.clip(unit_here, 0, unit_count - 1), 0, keepdims=False
        )
        current = jnp.where(position == 0, anchor, incoming)
        result = lax.cond(active, apply_layer, keep_input, current, anchor)
        outgoing = jnp.where(position == section_count - 1, result, outgoing)
        held_unit = moment + position - 2 * section_count + 2
        arrived = (
            (held_unit >= 0)
            & (held_unit < unit_count)
            & (held_unit // pieces % section_count == position)
        )
        held_safe = jnp.clip(held_unit, 0, unit_count - 1)
        slot_index = held_safe // pieces // section_count * pieces + held_safe % pieces
        previous = lax.dynamic_index_in_dim(collected, slot_index, 0, keepdims=False)
        collected = lax.dynamic_update_index_in_dim(
            collected, jnp.where(arrived, outgoing, previous), slot_index, 0
        )
        return (result, outgoing, collected)

    def forward_step(carried, moment):
        result, outgoing, collected = advance(carried, moment)
        incoming = from_behind(result, "section", 1)
        return ((incoming, outgoing, collected), None)

    def cycle_step(carried, moment):
        moved, _ = forward_step(carried, moment)
        incoming, outgoing, collected = moved
        outgoing = from_behind(outgoing, "section", -1)
        return ((incoming, outgoing, collected), None)

    blank = jnp.zeros((piece_rows, feature_count), jnp.bfloat16)
    holding = jnp.zeros((local_micro * pieces, piece_rows, feature_count), jnp.bfloat16)
    carried, _ = lax.scan(
        forward_step, (blank, blank, holding), jnp.arange(0, section_count - 1, dtype=jnp.int32)
    )
    carried, _ = lax.scan(
        cycle_step, carried, jnp.arange(section_count - 1, step_count - 1, dtype=jnp.int32)
    )
    _, _, collected = advance(carried, jnp.int32(step_count - 1))
    return collected.reshape(local_micro, 1, row_count, feature_count)


def solution(mesh):
    placed = (
        P(None, "section", "dp", None),
        P("section", None, None),
        P("section", None, None, None),
        P("section", None, None),
        P("section", None, None),
        P("section", None),
    )
    return jax.shard_map(
        per_device,
        mesh=mesh,
        in_specs=placed,
        out_specs=P(None, "section", "dp", None),
        check_vma=False,
    )
```

profile of v0, /device:TPU:2, one launch (start us, length us, event | category | flops | bytes accessed | tf_op | source)
XLA Modules:
  0.0 130.4 jit_solution(13214571090702250396)
XLA Ops:
  6.5 0.7 all-gather.2.cloned.1.call-update
  7.3 34.8 %all-gather.2.cloned.1.call-done = bf16[1,2,128,4096]{3,2,0,1:T(8,128)(2,1)} async-done(((bf16[1,1,128,4096]{3,2,0,1:T(8,128)(2,1)}), bf16[1,2,128,4096]{3,2,0,1:T(8,128)(2,1)}) %all-gather.2.cloned.1.call-update) | async-done | bytes 2097168 | tf_op jit(solution)/shard_map/all_gather | solution.py:43
  42.1 1.4 %broadcast_select_fusion.2 = (bf16[128,4096]{1,0:T(8,128)(2,1)S(1)}, bf16[128,4096]{1,0:T(8,128)(2,1)S(1)}) fusion(pred[]{:T(512)S(6)} %eq.38, bf16[1,2,128,4096]{3,2,0,1:T(8,128)(2,1)} %all-gather.2.cloned.1.call-done, s32[]{:T(128)S(6)} %min.19), kind=kLoop, calls=%fused_computation.48 | loop fusion | flops 524288 | bytes 3145733 | tf_op jit(solution)/shard_map/while/body/eval_jaxpr/jit(_where)/select_n | solution.py:66
  43.5 1.3 collective-permute-start
  44.8 32.0 %collective-permute-done = bf16[128,4096]{1,0:T(8,128)(2,1)} collective-permute-done((bf16[128,4096]{1,0:T(8,128)(2,1)S(1)}, bf16[128,4096]{1,0:T(8,128)(2,1)}, u32[]{:S(2)}, u32[]{:S(2)}) %collective-permute-start) | collective-permute-done | bytes 1048608 | tf_op jit(solution)/shard_map/while/body/eval_jaxpr/ppermute | solution.py:10
  76.8 1.7 %broadcast_select_fusion.1 = (bf16[128,4096]{1,0:T(8,128)(2,1)S(1)}, bf16[128,4096]{1,0:T(8,128)(2,1)S(1)}) fusion(bf16[128,4096]{1,0:T(8,128)(2,1)} %collective-permute-done, pred[]{:T(512)S(6)} %eq.38, bf16[1,2,128,4096]{3,2,0,1:T(8,128)(2,1)} %all-gather.2.cloned.1.call-done, s32[]{:T(128)S(6)} %min.18), kind=kLoop, calls=%fused_computation.47 | loop fusion | flops 524288 | bytes 4194309 | tf_op jit(solution)/shard_map/while/body/eval_jaxpr/jit(_where)/select_n | solution.py:66
  78.5 7.3 %conditional.4 = (bf16[128,4096]{1,0:T(8,128)(2,1)S(1)}) conditional(s32[]{:T(128)} %convert_element_type.57, bf16[128,4096]{1,0:T(8,128)(2,1)S(1)} %get-tuple-element.150, (bf16[128,4096]{1,0:T(8,128)(2,1)S(1)}, bf16[128,4096]{1,0:T(8,128)(2,1)S(1)}, bf16[2,4096]{1,0:T(2,128)(2,1)S(1)}, bf16[4096,512]{1,0:T(8,128)(2,1)}, ...), branch_computations={%region_3.4_spmd, %region_4.6_spmd} | conditional | flops 1112736768 | bytes 15767588 | solution.py:67
  78.5 3.0 %fusion.14 = bf16[128,512]{1,0:T(8,128)(2,1)S(1)} fusion(bf16[128,4096]{1,0:T(8,128)(2,1)S(1)} %get-tuple-element.134, bf16[4096,512]{1,0:T(8,128)(2,1)} %get-tuple-element.137), kind=kOutput, calls=%fused_computation.22 | convolution fusion | flops 536936448 | bytes 5373952 | tf_op jit(solution)/shard_map/while/body/eval_jaxpr/cond/branch_1_fun/dot_general | solution.py:17
  81.5 0.4 fusion.28
  82.0 0.2 fusion.15
  82.2 0.1 copy.44
  82.3 3.6 %fusion.11 = bf16[128,4096]{1,0:T(8,128)(2,1)S(1)} fusion(bf16[128,512]{0,1:T(8,128)(2,1)S(1)} %bitcast.81, bf16[512,4096]{1,0:T(8,128)(2,1)} %get-tuple-element.139, bf16[128,4096]{1,0:T(8,128)(2,1)S(1)} %get-tuple-element.135, bf16[128,4096]{1,0:T(8,128)(2,1)S(1)} %get-tuple-element.134, f32[4096]{0:T(1024)S(1)} %bitcast.87), kind=kOutput, calls=%fused_computation.17 | convolution fusion | flops 540016640 | bytes 7487488 | tf_op jit(solution)/shard_map/while/body/eval_jaxpr/cond/branch_1_fun/dot_general | solution.py:30
  85.9 1.3 collective-permute-start.1
  87.2 1.1 broadcast_select_fusion.3
  88.3 6.5 %collective-permute-start.2 = (bf16[128,4096]{1,0:T(8,128)(2,1)}, bf16[128,4096]{1,0:T(8,128)(2,1)}, u32[]{:S(2)}, u32[]{:S(2)}) collective-permute-start(bf16[128,4096]{1,0:T(8,128)(2,1)} %broadcast_select_fusion.3), channel_id=1, source_target_pairs={{16,0},{17,1},{18,2},{19,3},{20,4},{21,5},{22,6},{23,7},{24,8},{25... | collective-permute-start | bytes 3145736 | tf_op jit(solution)/shard_map/while/body/eval_jaxpr/ppermute | solution.py:10
  94.8 17.2 %collective-permute-done.1 = bf16[128,4096]{1,0:T(8,128)(2,1)} collective-permute-done((bf16[128,4096]{1,0:T(8,128)(2,1)S(1)}, bf16[128,4096]{1,0:T(8,128)(2,1)}, u32[]{:S(2)}, u32[]{:S(2)}) %collective-permute-start.1) | collective-permute-done | bytes 1048608 | tf_op jit(solution)/shard_map/while/body/eval_jaxpr/ppermute | solution.py:10
  112.0 2.6 %broadcast_select_fusion = (bf16[128,4096]{1,0:T(8,128)(2,1)S(1)}, bf16[128,4096]{1,0:T(8,128)(2,1)}) fusion(bf16[128,4096]{1,0:T(8,128)(2,1)} %collective-permute-done.1, pred[]{:T(512)S(6)} %eq.38, bf16[1,2,128,4096]{3,2,0,1:T(8,128)(2,1)} %all-gather.2.cloned.1.call-done, s32[]{:T(128)S(6)} %min.17), kind=kLoop, calls=%fused_computation.46 | loop fusion | flops 524288 | bytes 4194309 | tf_op jit(solution)/shard_map/jit(_where)/select_n | solution.py:66
  114.7 7.6 %conditional.5 = (bf16[128,4096]{1,0:T(8,128)(2,1)S(1)}) conditional(s32[]{:T(128)} %convert_element_type.56, bf16[128,4096]{1,0:T(8,128)(2,1)S(1)} %get-tuple-element.148, (bf16[128,4096]{1,0:T(8,128)(2,1)S(1)}, bf16[128,4096]{1,0:T(8,128)(2,1)}, bf16[2,4096]{1,0:T(2,128)(2,1)S(1)}, bf16[4096,512]{1,0:T(8,128)(2,1)}, bf16[2,256,256]{2,1,0:T(8,128)(2,1)}, ...), branch_computations={%region_6.7_spmd, %region_7.9_spmd} | conditional | flops 1112736768 | bytes 15767588 | solution.py:67
  114.7 3.0 %fusion.23 = bf16[128,512]{1,0:T(8,128)(2,1)S(1)} fusion(bf16[128,4096]{1,0:T(8,128)(2,1)S(1)} %get-tuple-element.141, bf16[4096,512]{1,0:T(8,128)(2,1)} %get-tuple-element.144), kind=kOutput, calls=%fused_computation.36 | convolution fusion | flops 536936448 | bytes 5373952 | tf_op jit(solution)/shard_map/cond/branch_1_fun/dot_general | solution.py:17
  117.7 0.4 fusion.29
  118.1 0.2 fusion.24
  118.3 0.1 copy.46
  118.4 3.9 %fusion.20 = bf16[128,4096]{1,0:T(8,128)(2,1)S(1)} fusion(bf16[128,512]{0,1:T(8,128)(2,1)S(1)} %bitcast.82, bf16[512,4096]{1,0:T(8,128)(2,1)} %get-tuple-element.146, bf16[128,4096]{1,0:T(8,128)(2,1)} %get-tuple-element.142, bf16[128,4096]{1,0:T(8,128)(2,1)S(1)} %get-tuple-element.141, f32[4096]{0:T(1024)S(1)} %bitcast.88), kind=kOutput, calls=%fused_computation.31 | convolution fusion | flops 540016640 | bytes 7487488 | tf_op jit(solution)/shard_map/cond/branch_1_fun/dot_general | solution.py:30
  122.3 1.2 select_bitcast_fusion
  (17 shorter events, 0.1 us)
Async XLA Ops:
  6.5 35.6 %all-gather.2.cloned.1.call-start = ((), (), s32[]{:S(2)}) async-start(), calls=%async_computation | async-start | bytes 3145728 | tf_op jit(solution)/shard_map/all_gather | solution.py:43
  6.5 36.9 %copy-start = (bf16[1,2,4096]{2,1,0:T(2,128)(2,1)S(1)}, bf16[1,2,4096]{2,1,0:T(2,128)(2,1)}, u32[]{:S(2)}) copy-start(bf16[1,2,4096]{2,1,0:T(2,128)(2,1)} %param.16) | copy-start | bytes 49156
  6.5 36.9 %copy-start.1 = (f32[1,4096]{1,0:T(1,128)S(1)}, f32[1,4096]{1,0:T(1,128)}, u32[]{:S(2)}) copy-start(f32[1,4096]{1,0:T(1,128)} %param.17) | copy-start | bytes 49156
  6.5 36.9 %copy-start.2 = (bf16[1,2,256,256]{3,2,1,0:T(8,128)(2,1)S(1)}, bf16[1,2,256,256]{3,2,1,0:T(8,128)(2,1)}, u32[]{:S(2)}) copy-start(bf16[1,2,256,256]{3,2,1,0:T(8,128)(2,1)} %param.14) | copy-start | bytes 786436
  43.5 33.3 %collective-permute-start = (bf16[128,4096]{1,0:T(8,128)(2,1)S(1)}, bf16[128,4096]{1,0:T(8,128)(2,1)}, u32[]{:S(2)}, u32[]{:S(2)}) collective-permute-start(bf16[128,4096]{1,0:T(8,128)(2,1)S(1)} %get-tuple-element.154), channel_id=1, source_target_pairs={{0,16},{1,17},{2,18},{3,19},{4,20},{5,21},{6,22},{7,23},{8,24},{9,... | collective-permute-start | bytes 3145736 | tf_op jit(solution)/shard_map/while/body/eval_jaxpr/ppermute | solution.py:10
  78.5 3.4 %copy-start.3 = (bf16[2,256,256]{2,1,0:T(8,128)(2,1)S(1)}, bf16[2,256,256]{2,1,0:T(8,128)(2,1)}, u32[]{:S(2)}) copy-start(bf16[2,256,256]{2,1,0:T(8,128)(2,1)} %get-tuple-element.138) | copy-start | bytes 786436 | tf_op jit(solution)/shard_map/while/body/eval_jaxpr/cond
  85.9 26.2 %collective-permute-start.1 = (bf16[128,4096]{1,0:T(8,128)(2,1)S(1)}, bf16[128,4096]{1,0:T(8,128)(2,1)}, u32[]{:S(2)}, u32[]{:S(2)}) collective-permute-start(bf16[128,4096]{1,0:T(8,128)(2,1)S(1)} %get-tuple-element.155), channel_id=1, source_target_pairs={{0,16},{1,17},{2,18},{3,19},{4,20},{5,21},{6,22},{7,23},{8,24},{9,... | collective-permute-start | bytes 3145736 | tf_op jit(solution)/shard_map/while/body/eval_jaxpr/ppermute | solution.py:10
  88.3 34.0 %collective-permute-start.2 = (bf16[128,4096]{1,0:T(8,128)(2,1)}, bf16[128,4096]{1,0:T(8,128)(2,1)}, u32[]{:S(2)}, u32[]{:S(2)}) collective-permute-start(bf16[128,4096]{1,0:T(8,128)(2,1)} %broadcast_select_fusion.3), channel_id=1, source_target_pairs={{16,0},{17,1},{18,2},{19,3},{20,4},{21,5},{22,6},{23,7},{24,8},{25... | collective-permute-start | bytes 3145736 | tf_op jit(solution)/shard_map/while/body/eval_jaxpr/ppermute | solution.py:10
  114.7 3.4 %copy-start.4 = (bf16[2,256,256]{2,1,0:T(8,128)(2,1)S(1)}, bf16[2,256,256]{2,1,0:T(8,128)(2,1)}, u32[]{:S(2)}) copy-start(bf16[2,256,256]{2,1,0:T(8,128)(2,1)} %get-tuple-element.145) | copy-start | bytes 786436 | tf_op jit(solution)/shard_map/cond
Sparse Core Ops, SparseCore 0:
  8.9 33.1 all-gather.1
where the time goes:
time: 131 us; the launch traced here: 130 us
  waiting for transfers between devices  84.8 us (65%)
  matrix products  14.5 us (11%)
  between operations  13.5 us (10%)
  starting transfers between devices  9.1 us (7%)
  other arithmetic  8.06 us (6%)
    ppermute x3, waiting for transfers between devices, from_behind(): return lax.ppermute(block, axis, route)  49.3 us
    all_gather x1, waiting for transfers between devices, per_device(): everyone = lax.all_gather(features, 'section', axis=1, tiled=True)  34.8 us
    ppermute x3, starting transfers between devices, from_behind(): return lax.ppermute(block, axis, route)  9.1 us
    dot_general x2, matrix products, cross_layer(): crossed = jnp.dot(blended, u_mat, preferred_element_type=jnp.float32)  7.47 us
    dot_general x2, matrix products, cross_layer(): projected = jnp.dot(current, v_mat, preferred_element_type=jnp.float32)  5.91 us
    select_n x3, other arithmetic, advance(): current = jnp.where(position == 0, anchor, incoming)  5.69 us
  transfers between devices with their start and end apart: 4, of which 3 were waited for; matrix products, arithmetic and copies ran while one was open for 9% of the time, Pallas kernels for 0%

commit v1 on v0

--- a/solution.py
+++ b/solution.py
@@ -2,6 +2,9 @@
 import jax.numpy as jnp
 from jax import lax
 from jax.sharding import PartitionSpec as P
+
+
+PIECES = 2
 
 
 def from_behind(block, axis, distance):
@@ -10,7 +13,7 @@
     return lax.ppermute(block, axis, route)
 
 
-def cross_layer(current, anchor, v_mat, c_mat, u_mat, gate_mat, shift_row):
+def blend(current, v_mat, c_mat, gate_mat):
     row_count = current.shape[0]
     expert_count = c_mat.shape[0]
     rank_size = c_mat.shape[1]
@@ -26,13 +29,24 @@
     )
     gate_values = 1.0 / jnp.sum(jnp.exp(logits[:, None, :] - logits[:, :, None]), axis=2)
     blended = (gate_values[:, :, None] * jnp.tanh(inner_second)).astype(jnp.bfloat16)
-    blended = blended.reshape(row_count, expert_count * rank_size)
-    crossed = jnp.dot(blended, u_mat, preferred_element_type=jnp.float32)
-    updated = current.astype(jnp.float32) + anchor.astype(jnp.float32) * (crossed + shift_row)
-    return updated.astype(jnp.bfloat16)
+    return blended.reshape(row_count, expert_count * rank_size)
 
 
-def per_device(features, in_proj, mix_proj, out_proj, gate_proj, cross_bias):
+def shifted_cross(blended, u_mat, shift_row):
+    return jnp.dot(blended, u_mat, preferred_element_type=jnp.float32) + shift_row
+
+
+def updated(current, anchor, moved):
+    wide = current.astype(jnp.float32) + anchor.astype(jnp.float32) * moved.astype(jnp.float32)
+    return wide.astype(jnp.bfloat16)
+
+
+def cross_layer(current, anchor, v_mat, c_mat, u_mat, gate_mat, shift_row):
+    blended = blend(current, v_mat, c_mat, gate_mat)
+    return updated(current, anchor, shifted_cross(blended, u_mat, shift_row))
+
+
+def relay_many(features, in_proj, mix_proj, out_proj, gate_proj, cross_bias):
     section_count = lax.axis_size("section")
     position = lax.axis_index("section")
     pieces = 1
@@ -103,6 +117,43 @@
     return collected.reshape(local_micro, 1, row_count, feature_count)
 
 
+def swap(block):
+    return lax.ppermute(block, "section", [(0, 1), (1, 0)])
+
+
+def pair_exchange(features, in_proj, mix_proj, out_proj, gate_proj, cross_bias):
+    first_section = lax.axis_index("section") == 0
+    local_micro, _, row_count, feature_count = features.shape
+    rows = local_micro * row_count
+    x0 = features.reshape(rows, feature_count)
+    v_mat, c_mat, u_mat = in_proj[0], mix_proj[0], out_proj[0]
+    gate_mat, shift_row = gate_proj[0], cross_bias[0]
+    pieces = PIECES if rows % (16 * PIECES) == 0 else 1
+    size = rows // pieces
+    anchors = [x0[i * size : (i + 1) * size] for i in range(pieces)]
+    sent, got = [], []
+    for anchor in anchors:
+        after = cross_layer(anchor, anchor, v_mat, c_mat, u_mat, gate_mat, shift_row)
+        sent.append(jnp.where(first_section, after, anchor))
+        got.append(swap(sent[-1]))
+    back = []
+    for block in got:
+        moved = shifted_cross(blend(block, v_mat, c_mat, gate_mat), u_mat, shift_row)
+        back.append(swap(moved.astype(jnp.bfloat16)))
+    finished = []
+    for anchor, current, moved in zip(anchors, sent, back):
+        current = updated(current, anchor, moved)
+        after = cross_layer(current, anchor, v_mat, c_mat, u_mat, gate_mat, shift_row)
+        finished.append(jnp.where(first_section, current, after))
+    return jnp.concatenate(finished, axis=0).reshape(features.shape)
+
+
+def per_device(*arrays):
+    if lax.axis_size("section") == 2:
+        return pair_exchange(*arrays)
+    return relay_many(*arrays)
+
+
 def solution(mesh):
     placed = (
         P(None, "section", "dp", None),

time: 131 us -> 63.4 us (0.48)
  the two profiles are of different devices: /device:TPU:2 before, /device:TPU:0 now
where the time goes in v1:
time: 63.4 us; the launch traced here: 63.2 us
  waiting for transfers between devices  33.9 us (53%)
  matrix products  19.2 us (30%)
  starting transfers between devices  8.07 us (13%)
  other arithmetic  1.72 us (3%)
    ppermute x4, waiting for transfers between devices, swap(): return lax.ppermute(block, 'section', [(0, 1), (1, 0)])  33.9 us
    ppermute x4, starting transfers between devices, swap(): return lax.ppermute(block, 'section', [(0, 1), (1, 0)])  8.07 us
    dot_general x6, matrix products, shifted_cross(): jnp.dot(blended, u_mat, preferred_element_type=jnp.float32) + shift_row  8.02 us
    dot_general x6, matrix products, blend(): projected = jnp.dot(current, v_mat, preferred_element_type=jnp.float32)  7.49 us
    dot_general x6, matrix products, blend(): lax.dot_general(current, gate_mat, (((1,), (1,)), ((), ())), preferred_el...  2.57 us
  transfers between devices with their start and end apart: 4, of which 4 were waited for; matrix products, arithmetic and copies ran while one was open for 10% of the time, Pallas kernels for 0%

profile of v1, /device:TPU:0, one launch (start us, length us, event | category | flops | bytes accessed | tf_op | source)
XLA Modules:
  0.0 63.2 jit_solution(14647276520374856189)
XLA Ops:
  0.0 1.4 %fusion.97 = f32[64,2]{0,1:T(2,128)S(1)} fusion(bf16[1,1,128,4096]{3,2,1,0:T(8,128)(2,1)} %param.6, bf16[1,2,4096]{2,1,0:T(2,128)(2,1)} %param.10), kind=kOutput, calls=%fused_computation.90 | convolution fusion | flops 1048576 | bytes 541184 | tf_op jit(solution)/shard_map/dot_general | solution.py:27
  1.5 3.2 %fusion.72 = bf16[64,512]{1,0:T(8,128)(2,1)S(1)} fusion(bf16[1,4096,512]{2,1,0:T(8,128)(2,1)} %param.7, bf16[1,1,128,4096]{3,2,1,0:T(8,128)(2,1)} %param.6), kind=kOutput, calls=%fused_computation.70 | convolution fusion | flops 268468224 | bytes 4784128 | tf_op jit(solution)/shard_map/dot_general | solution.py:20
  4.9 3.3 %fusion.10 = bf16[64,4096]{1,0:T(8,128)(2,1)S(1)} fusion(bf16[64,512]{1,0:T(8,128)(2,1)S(1)} %bitcast.213, bf16[1,512,4096]{2,1,0:T(8,128)(2,1)} %param.9, f32[4096]{0:T(1024)S(1)} %bitcast.207, pred[]{:T(512)S(6)} %eq.3, bf16[1,1,128,4096]{3,2,1,0:T(8,128)(2,1)S(1)} %copy-done.3), kind=kOutput, calls=%fused_computation.16 | convolution fusion | flops 270008320 | bytes 5324801 | tf_op jit(solution)/shard_map/dot_general | solution.py:36
  8.2 3.0 %collective-permute-start.2 = (bf16[64,4096]{1,0:T(8,128)(2,1)S(1)}, bf16[64,4096]{1,0:T(8,128)(2,1)S(1)}, u32[]{:S(2)}, u32[]{:S(2)}) collective-permute-start(bf16[64,4096]{1,0:T(8,128)(2,1)S(1)} %fusion.10), channel_id=1, source_target_pairs={{0,16},{16,0},{1,17},{17,1},{2,18},{18,2},{3,19},{19,3},{4,20},{20... | collective-permute-start | bytes 1572872 | tf_op jit(solution)/shard_map/ppermute | solution.py:121
  11.5 0.9 %fusion.81 = bf16[64,512]{1,0:T(8,128)(2,1)S(1)} fusion(bf16[1,4096,512]{2,1,0:T(8,128)(2,1)S(1)} %copy-done.1, bf16[1,1,128,4096]{3,2,1,0:T(8,128)(2,1)S(1)} %copy-done.3), kind=kOutput, calls=%fused_computation.73 | convolution fusion | flops 268468224 | bytes 4784128 | tf_op jit(solution)/shard_map/dot_general | solution.py:20
  12.6 1.0 %fusion.11 = bf16[64,4096]{1,0:T(8,128)(2,1)S(1)} fusion(bf16[64,512]{1,0:T(8,128)(2,1)S(1)} %bitcast.216, bf16[1,512,4096]{2,1,0:T(8,128)(2,1)S(1)} %copy-done.2, f32[4096]{0:T(1024)S(1)} %bitcast.208, pred[]{:T(512)S(6)} %eq.3, bf16[1,1,128,4096]{3,2,1,0:T(8,128)(2,1)S(1)} %copy-done.3), kind=kOutput, calls=%fused_computation.17 | convolution fusion | flops 270008320 | bytes 5324801 | tf_op jit(solution)/shard_map/dot_general | solution.py:36
  13.6 0.8 %collective-permute-start = (bf16[64,4096]{1,0:T(8,128)(2,1)S(1)}, bf16[64,4096]{1,0:T(8,128)(2,1)S(1)}, u32[]{:S(2)}, u32[]{:S(2)}) collective-permute-start(bf16[64,4096]{1,0:T(8,128)(2,1)S(1)} %fusion.11), channel_id=1, source_target_pairs={{0,16},{16,0},{1,17},{17,1},{2,18},{18,2},{3,19},{19,3},{4,20},{20... | collective-permute-start | bytes 1572872 | tf_op jit(solution)/shard_map/ppermute | solution.py:121
  14.4 9.6 %collective-permute-done.2 = bf16[64,4096]{1,0:T(8,128)(2,1)S(1)} collective-permute-done((bf16[64,4096]{1,0:T(8,128)(2,1)S(1)}, bf16[64,4096]{1,0:T(8,128)(2,1)S(1)}, u32[]{:S(2)}, u32[]{:S(2)}) %collective-permute-start.2) | collective-permute-done | bytes 524320 | tf_op jit(solution)/shard_map/ppermute | solution.py:121
  24.3 0.8 %fusion.69 = bf16[64,512]{1,0:T(8,128)(2,1)S(1)} fusion(bf16[64,4096]{1,0:T(8,128)(2,1)S(1)} %collective-permute-done.2, bf16[1,4096,512]{2,1,0:T(8,128)(2,1)S(1)} %copy-done.1), kind=kOutput, calls=%fused_computation.69 | convolution fusion | flops 268468224 | bytes 4784128 | tf_op jit(solution)/shard_map/dot_general | solution.py:20
  25.4 0.8 %fusion.9 = bf16[64,4096]{1,0:T(8,128)(2,1)S(1)} fusion(bf16[64,512]{1,0:T(8,128)(2,1)S(1)} %bitcast.217, bf16[1,512,4096]{2,1,0:T(8,128)(2,1)S(1)} %copy-done.2, f32[4096]{0:T(1024)S(1)} %bitcast.209), kind=kOutput, calls=%fused_computation.15 | convolution fusion | flops 268959744 | bytes 4800512 | tf_op jit(solution)/shard_map/dot_general | solution.py:36
  26.2 2.1 %collective-permute-start.3 = (bf16[64,4096]{1,0:T(8,128)(2,1)S(1)}, bf16[64,4096]{1,0:T(8,128)(2,1)S(1)}, u32[]{:S(2)}, u32[]{:S(2)}) collective-permute-start(bf16[64,4096]{1,0:T(8,128)(2,1)S(1)} %fusion.9), channel_id=1, source_target_pairs={{0,16},{16,0},{1,17},{17,1},{2,18},{18,2},{3,19},{19,3},{4,20},{20... | collective-permute-start | bytes 1572872 | tf_op jit(solution)/shard_map/ppermute | solution.py:121
  28.3 6.9 %collective-permute-done = bf16[64,4096]{1,0:T(8,128)(2,1)S(1)} collective-permute-done((bf16[64,4096]{1,0:T(8,128)(2,1)S(1)}, bf16[64,4096]{1,0:T(8,128)(2,1)S(1)}, u32[]{:S(2)}, u32[]{:S(2)}) %collective-permute-start) | collective-permute-done | bytes 524320 | tf_op jit(solution)/shard_map/ppermute | solution.py:121
  35.6 0.8 %fusion.78 = bf16[64,512]{1,0:T(8,128)(2,1)S(1)} fusion(bf16[64,4096]{1,0:T(8,128)(2,1)S(1)} %collective-permute-done, bf16[1,4096,512]{2,1,0:T(8,128)(2,1)S(1)} %copy-done.1), kind=kOutput, calls=%fused_computation.72 | convolution fusion | flops 268468224 | bytes 4784128 | tf_op jit(solution)/shard_map/dot_general | solution.py:20
  36.6 0.8 %fusion.7 = bf16[64,4096]{1,0:T(8,128)(2,1)S(1)} fusion(bf16[64,512]{1,0:T(8,128)(2,1)S(1)} %bitcast.218, bf16[1,512,4096]{2,1,0:T(8,128)(2,1)S(1)} %copy-done.2, f32[4096]{0:T(1024)S(1)} %bitcast.210), kind=kOutput, calls=%fused_computation.13 | convolution fusion | flops 268959744 | bytes 4800512 | tf_op jit(solution)/shard_map/dot_general | solution.py:36
  37.5 2.1 %collective-permute-start.1 = (bf16[64,4096]{1,0:T(8,128)(2,1)S(1)}, bf16[64,4096]{1,0:T(8,128)(2,1)S(1)}, u32[]{:S(2)}, u32[]{:S(2)}) collective-permute-start(bf16[64,4096]{1,0:T(8,128)(2,1)S(1)} %fusion.7), channel_id=1, source_target_pairs={{0,16},{16,0},{1,17},{17,1},{2,18},{18,2},{3,19},{19,3},{4,20},{20... | collective-permute-start | bytes 1572872 | tf_op jit(solution)/shard_map/ppermute | solution.py:121
  39.6 6.9 %collective-permute-done.3 = bf16[64,4096]{1,0:T(8,128)(2,1)S(1)} collective-permute-done((bf16[64,4096]{1,0:T(8,128)(2,1)S(1)}, bf16[64,4096]{1,0:T(8,128)(2,1)S(1)}, u32[]{:S(2)}, u32[]{:S(2)}) %collective-permute-start.3) | collective-permute-done | bytes 524320 | tf_op jit(solution)/shard_map/ppermute | solution.py:121
  46.5 10.4 %collective-permute-done.1 = bf16[64,4096]{1,0:T(8,128)(2,1)S(1)} collective-permute-done((bf16[64,4096]{1,0:T(8,128)(2,1)S(1)}, bf16[64,4096]{1,0:T(8,128)(2,1)S(1)}, u32[]{:S(2)}, u32[]{:S(2)}) %collective-permute-start.1) | collective-permute-done | bytes 524320 | tf_op jit(solution)/shard_map/ppermute | solution.py:121
  56.9 0.5 fusion.91
  57.4 0.2 fusion.133
  57.6 0.9 %fusion.75 = bf16[64,512]{1,0:T(8,128)(2,1)S(1)} fusion(bf16[64,4096]{1,0:T(8,128)(2,1)S(1)} %get-tuple-element.5, bf16[1,4096,512]{2,1,0:T(8,128)(2,1)S(1)} %copy-done.1), kind=kOutput, calls=%fused_computation.71 | convolution fusion | flops 268468224 | bytes 4784128 | tf_op jit(solution)/shard_map/dot_general | solution.py:20
  58.7 0.9 %fusion.66 = bf16[64,512]{1,0:T(8,128)(2,1)S(1)} fusion(bf16[64,4096]{1,0:T(8,128)(2,1)S(1)} %get-tuple-element.6, bf16[1,4096,512]{2,1,0:T(8,128)(2,1)S(1)} %copy-done.1), kind=kOutput, calls=%fused_computation.68 | convolution fusion | flops 268468224 | bytes 4784128 | tf_op jit(solution)/shard_map/dot_general | solution.py:20
  59.9 1.1 %fusion.94 = bf16[64,4096]{1,0:T(8,128)(2,1)S(1)} fusion(bf16[64,4096]{1,0:T(8,128)(2,1)S(1)} %get-tuple-element.5, bf16[64,512]{1,0:T(8,128)(2,1)S(1)} %bitcast.215, bf16[1,512,4096]{2,1,0:T(8,128)(2,1)S(1)} %copy-done.2, f32[4096]{0:T(1024)S(1)} %bitcast.211, pred[]{:T(512)S(6)} %eq.3, bf16[1,1,128,4096]{3,2,1,0:T(8,128)(2,1)S(1)} %copy-done.3), kind=kOutput, calls=%fused_computation.87 | convolution fusion | flops 270270464 | bytes 5849089 | tf_op jit(solution)/shard_map/dot_general | solution.py:36
  61.1 1.1 %fusion.95 = bf16[64,4096]{1,0:T(8,128)(2,1)S(1)} fusion(bf16[64,4096]{1,0:T(8,128)(2,1)S(1)} %get-tuple-element.6, bf16[64,512]{1,0:T(8,128)(2,1)S(1)} %bitcast.214, bf16[1,512,4096]{2,1,0:T(8,128)(2,1)S(1)} %copy-done.2, f32[4096]{0:T(1024)S(1)} %bitcast.212, pred[]{:T(512)S(6)} %eq.3, bf16[1,1,128,4096]{3,2,1,0:T(8,128)(2,1)S(1)} %copy-done.3), kind=kOutput, calls=%fused_computation.88 | convolution fusion | flops 270270464 | bytes 5849089 | tf_op jit(solution)/shard_map/dot_general | solution.py:36
  62.2 1.0 %maximum_bitcast_fusion = bf16[1,1,128,4096]{3,2,1,0:T(8,128)(2,1)} fusion(bf16[64,4096]{1,0:T(8,128)(2,1)S(1)} %fusion.95, bf16[64,4096]{1,0:T(8,128)(2,1)S(1)} %fusion.94), kind=kLoop, calls=%fused_computation.84 | loop fusion | flops 2097152 | bytes 2097152 | tf_op jit(solution)/shard_map/reshape | solution.py:148
  (40 shorter events, 2.3 us)
Async XLA Ops:
  0.0 4.7 %copy-start = (bf16[1,2,256,256]{3,2,1,0:T(8,128)(2,1)S(1)}, bf16[1,2,256,256]{3,2,1,0:T(8,128)(2,1)}, u32[]{:S(2)}) copy-start(bf16[1,2,256,256]{3,2,1,0:T(8,128)(2,1)} %param.8) | copy-start | bytes 786436
  0.0 4.9 %copy-start.3 = (bf16[1,1,128,4096]{3,2,1,0:T(8,128)(2,1)S(1)}, bf16[1,1,128,4096]{3,2,1,0:T(8,128)(2,1)}, u32[]{:S(2)}) copy-start(bf16[1,1,128,4096]{3,2,1,0:T(8,128)(2,1)} %param.6) | copy-start | bytes 3145732
  0.0 4.9 %copy-start.4 = (f32[1,4096]{1,0:T(1,128)S(1)}, f32[1,4096]{1,0:T(1,128)}, u32[]{:S(2)}) copy-start(f32[1,4096]{1,0:T(1,128)} %param.11) | copy-start | bytes 49156
  1.4 9.8 %copy-start.5 = (bf16[1,2,4096]{2,1,0:T(2,128)(2,1)S(1)}, bf16[1,2,4096]{2,1,0:T(2,128)(2,1)}, u32[]{:S(2)}) copy-start(bf16[1,2,4096]{2,1,0:T(2,128)(2,1)} %param.10) | copy-start | bytes 49156
  4.9 6.6 %copy-start.1 = (bf16[1,4096,512]{2,1,0:T(8,128)(2,1)S(1)}, bf16[1,4096,512]{2,1,0:T(8,128)(2,1)}, u32[]{:S(2)}) copy-start(bf16[1,4096,512]{2,1,0:T(8,128)(2,1)} %param.7) | copy-start | bytes 12582916
  8.2 4.4 %copy-start.2 = (bf16[1,512,4096]{2,1,0:T(8,128)(2,1)S(1)}, bf16[1,512,4096]{2,1,0:T(8,128)(2,1)}, u32[]{:S(2)}) copy-start(bf16[1,512,4096]{2,1,0:T(8,128)(2,1)} %param.9) | copy-start | bytes 12582916
  8.2 15.8 %collective-permute-start.2 = (bf16[64,4096]{1,0:T(8,128)(2,1)S(1)}, bf16[64,4096]{1,0:T(8,128)(2,1)S(1)}, u32[]{:S(2)}, u32[]{:S(2)}) collective-permute-start(bf16[64,4096]{1,0:T(8,128)(2,1)S(1)} %fusion.10), channel_id=1, source_target_pairs={{0,16},{16,0},{1,17},{17,1},{2,18},{18,2},{3,19},{19,3},{4,20},{20... | collective-permute-start | bytes 1572872 | tf_op jit(solution)/shard_map/ppermute | solution.py:121
  13.6 21.7 %collective-permute-start = (bf16[64,4096]{1,0:T(8,128)(2,1)S(1)}, bf16[64,4096]{1,0:T(8,128)(2,1)S(1)}, u32[]{:S(2)}, u32[]{:S(2)}) collective-permute-start(bf16[64,4096]{1,0:T(8,128)(2,1)S(1)} %fusion.11), channel_id=1, source_target_pairs={{0,16},{16,0},{1,17},{17,1},{2,18},{18,2},{3,19},{19,3},{4,20},{20... | collective-permute-start | bytes 1572872 | tf_op jit(solution)/shard_map/ppermute | solution.py:121
  26.2 20.3 %collective-permute-start.3 = (bf16[64,4096]{1,0:T(8,128)(2,1)S(1)}, bf16[64,4096]{1,0:T(8,128)(2,1)S(1)}, u32[]{:S(2)}, u32[]{:S(2)}) collective-permute-start(bf16[64,4096]{1,0:T(8,128)(2,1)S(1)} %fusion.9), channel_id=1, source_target_pairs={{0,16},{16,0},{1,17},{17,1},{2,18},{18,2},{3,19},{19,3},{4,20},{20... | collective-permute-start | bytes 1572872 | tf_op jit(solution)/shard_map/ppermute | solution.py:121
  37.5 19.4 %collective-permute-start.1 = (bf16[64,4096]{1,0:T(8,128)(2,1)S(1)}, bf16[64,4096]{1,0:T(8,128)(2,1)S(1)}, u32[]{:S(2)}, u32[]{:S(2)}) collective-permute-start(bf16[64,4096]{1,0:T(8,128)(2,1)S(1)} %fusion.7), channel_id=1, source_target_pairs={{0,16},{16,0},{1,17},{17,1},{2,18},{18,2},{3,19},{19,3},{4,20},{20... | collective-permute-start | bytes 1572872 | tf_op jit(solution)/shard_map/ppermute | solution.py:121

commit v2 on v1

--- a/solution.py
+++ b/solution.py
@@ -4,7 +4,7 @@
 from jax.sharding import PartitionSpec as P
 
 
-PIECES = 2
+CUTS = (6,13)
 
 
 def from_behind(block, axis, distance):
@@ -128,9 +128,8 @@
     x0 = features.reshape(rows, feature_count)
     v_mat, c_mat, u_mat = in_proj[0], mix_proj[0], out_proj[0]
     gate_mat, shift_row = gate_proj[0], cross_bias[0]
-    pieces = PIECES if rows % (16 * PIECES) == 0 else 1
-    size = rows // pieces
-    anchors = [x0[i * size : (i + 1) * size] for i in range(pieces)]
+    cuts = [0] + [rows * part // 16 // 8 * 8 for part in CUTS] + [rows]
+    anchors = [x0[low:high] for low, high in zip(cuts, cuts[1:]) if high > low]
     sent, got = [], []
     for anchor in anchors:
         after = cross_layer(anchor, anchor, v_mat, c_mat, u_mat, gate_mat, shift_row)

time: 63.4 us -> 59.9 us (0.945)
  waiting for transfers between devices: 33.9 us -> 24 us
  matrix products: 19.2 us -> 23.5 us
  starting transfers between devices: 8.07 us -> 9.93 us
    ppermute x4 -> x6, waiting for transfers between devices: 33.9 us -> 24 us  [swap(): return lax.ppermute(block, 'section', [(0, 1), (1, 0)])]
    ppermute x4 -> x6, starting transfers between devices: 8.07 us -> 9.93 us  [swap(): return lax.ppermute(block, 'section', [(0, 1), (1, 0)])]
    dot_general x6 -> x9, matrix products: 7.49 us -> 9.3 us  [blend(): projected = jnp.dot(current, v_mat, preferred_element_type=jnp.float32)]
    dot_general x6 -> x9, matrix products: 8.02 us -> 9.81 us  [shifted_cross(): jnp.dot(blended, u_mat, preferred_element_type=jnp.float32) + shift_row]
    dot_general x6 -> x9, matrix products: 1.08 us -> 1.52 us  [blend(): jnp.einsum('rek,ekj->rej', inner_first, c_mat, preferred_element_type=jnp...]
    dot_general x6 -> x9, matrix products: 2.57 us -> 2.86 us  [blend(): lax.dot_general(current, gate_mat, (((1,), (1,)), ((), ())), preferred_el...]
  transfers between devices with their start and end apart: 4 -> 6, of which waited for: 4 -> 5; matrix products, arithmetic and copies ran while one was open for 10% -> 24% of each run, Pallas kernels for 0% -> 0%
where the time goes in v2:
time: 59.9 us; the launch traced here: 59.7 us
  waiting for transfers between devices  24 us (40%)
  matrix products  23.5 us (39%)
  starting transfers between devices  9.93 us (17%)
  other arithmetic  1.74 us (3%)
    ppermute x6, waiting for transfers between devices, swap(): return lax.ppermute(block, 'section', [(0, 1), (1, 0)])  24 us
    ppermute x6, starting transfers between devices, swap(): return lax.ppermute(block, 'section', [(0, 1), (1, 0)])  9.93 us
    dot_general x9, matrix products, shifted_cross(): jnp.dot(blended, u_mat, preferred_element_type=jnp.float32) + shift_row  9.81 us
    dot_general x9, matrix products, blend(): projected = jnp.dot(current, v_mat, preferred_element_type=jnp.float32)  9.3 us
    dot_general x9, matrix products, blend(): lax.dot_general(current, gate_mat, (((1,), (1,)), ((), ())), preferred_el...  2.86 us
    dot_general x9, matrix products, blend(): jnp.einsum('rek,ekj->rej', inner_first, c_mat, preferred_element_type=jnp...  1.52 us
  transfers between devices with their start and end apart: 6, of which 5 were waited for; matrix products, arithmetic and copies ran while one was open for 24% of the time, Pallas kernels for 0%

profile of v2, /device:TPU:0, one launch (start us, length us, event | category | flops | bytes accessed | tf_op | source)
XLA Modules:
  0.0 59.7 jit_solution(5258502550986059703)
XLA Ops:
  0.0 1.2 %fusion.168 = f32[24,2]{0,1:T(2,128)S(1)} fusion(bf16[1,1,128,4096]{3,2,1,0:T(8,128)(2,1)} %param.6, bf16[1,2,4096]{2,1,0:T(2,128)(2,1)} %param.10), kind=kOutput, calls=%fused_computation.153 | convolution fusion | flops 393216 | bytes 213184 | tf_op jit(solution)/shard_map/dot_general | solution.py:27
  1.3 3.0 %fusion.129 = bf16[24,512]{1,0:T(8,128)(2,1)S(1)} fusion(bf16[1,4096,512]{2,1,0:T(8,128)(2,1)} %param.7, bf16[1,1,128,4096]{3,2,1,0:T(8,128)(2,1)} %param.6), kind=kOutput, calls=%fused_computation.115 | convolution fusion | flops 100675584 | bytes 4415488 | tf_op jit(solution)/shard_map/dot_general | solution.py:20
  4.5 3.0 %fusion.17 = bf16[24,4096]{1,0:T(8,128)(2,1)S(1)} fusion(bf16[24,512]{1,0:T(8,128)(2,1)S(1)} %bitcast.332, bf16[1,512,4096]{2,1,0:T(8,128)(2,1)} %param.9, f32[4096]{0:T(1024)S(1)} %bitcast.307, pred[]{:T(512)S(6)} %eq.3, bf16[1,1,128,4096]{3,2,1,0:T(8,128)(2,1)S(1)} %copy-done.3), kind=kOutput, calls=%fused_computation.26 | convolution fusion | flops 101253120 | bytes 4628481 | tf_op jit(solution)/shard_map/dot_general | solution.py:36
  7.5 3.0 %collective-permute-start.4 = (bf16[24,4096]{1,0:T(8,128)(2,1)S(1)}, bf16[24,4096]{1,0:T(8,128)(2,1)S(1)}, u32[]{:S(2)}, u32[]{:S(2)}) collective-permute-start(bf16[24,4096]{1,0:T(8,128)(2,1)S(1)} %fusion.17), channel_id=1, source_target_pairs={{0,16},{16,0},{1,17},{17,1},{2,18},{18,2},{3,19},{19,3},{4,20},{20... | collective-permute-start | bytes 589832 | tf_op jit(solution)/shard_map/ppermute | solution.py:121
  10.8 0.8 %fusion.93 = bf16[48,512]{1,0:T(8,128)(2,1)S(1)} fusion(bf16[1,4096,512]{2,1,0:T(8,128)(2,1)S(1)} %copy-done.1, bf16[1,1,128,4096]{3,2,1,0:T(8,128)(2,1)S(1)} %copy-done.3), kind=kOutput, calls=%fused_computation.88 | convolution fusion | flops 201351168 | bytes 4636672 | tf_op jit(solution)/shard_map/dot_general | solution.py:20
  11.9 0.9 %fusion.11 = bf16[48,4096]{1,0:T(8,128)(2,1)S(1)} fusion(bf16[48,512]{1,0:T(8,128)(2,1)S(1)} %bitcast.327, bf16[1,512,4096]{2,1,0:T(8,128)(2,1)S(1)} %copy-done.2, f32[4096]{0:T(1024)S(1)} %bitcast.308, pred[]{:T(512)S(6)} %eq.3, bf16[1,1,128,4096]{3,2,1,0:T(8,128)(2,1)S(1)} %copy-done.3), kind=kOutput, calls=%fused_computation.17 | convolution fusion | flops 202506240 | bytes 5046273 | tf_op jit(solution)/shard_map/dot_general | solution.py:36
  13.4 0.8 %fusion.81 = bf16[56,512]{1,0:T(8,128)(2,1)S(1)} fusion(bf16[1,4096,512]{2,1,0:T(8,128)(2,1)S(1)} %copy-done.1, bf16[1,1,128,4096]{3,2,1,0:T(8,128)(2,1)S(1)} %copy-done.3), kind=kOutput, calls=%fused_computation.82 | convolution fusion | flops 234909696 | bytes 4710400 | tf_op jit(solution)/shard_map/dot_general | solution.py:20
  14.4 1.5 %collective-permute-done.4 = bf16[24,4096]{1,0:T(8,128)(2,1)S(1)} collective-permute-done((bf16[24,4096]{1,0:T(8,128)(2,1)S(1)}, bf16[24,4096]{1,0:T(8,128)(2,1)S(1)}, u32[]{:S(2)}, u32[]{:S(2)}) %collective-permute-start.4) | collective-permute-done | bytes 196640 | tf_op jit(solution)/shard_map/ppermute | solution.py:121
  17.7 2.5 %collective-permute-start.5 = (bf16[24,4096]{1,0:T(8,128)(2,1)S(1)}, bf16[24,4096]{1,0:T(8,128)(2,1)S(1)}, u32[]{:S(2)}, u32[]{:S(2)}) collective-permute-start(bf16[24,4096]{1,0:T(8,128)(2,1)S(1)} %fusion.16), channel_id=1, source_target_pairs={{0,16},{16,0},{1,17},{17,1},{2,18},{18,2},{3,19},{19,3},{4,20},{20... | collective-permute-start | bytes 589832 | tf_op jit(solution)/shard_map/ppermute | solution.py:121
  20.1 0.9 %fusion.10 = bf16[56,4096]{1,0:T(8,128)(2,1)S(1)} fusion(bf16[56,512]{1,0:T(8,128)(2,1)S(1)} %bitcast.316, bf16[1,512,4096]{2,1,0:T(8,128)(2,1)S(1)} %copy-done.2, f32[4096]{0:T(1024)S(1)} %bitcast.310, pred[]{:T(512)S(6)} %eq.3, bf16[1,1,128,4096]{3,2,1,0:T(8,128)(2,1)S(1)} %copy-done.3), kind=kOutput, calls=%fused_computation.16 | convolution fusion | flops 236257280 | bytes 5185537 | tf_op jit(solution)/shard_map/dot_general | solution.py:36
  21.1 7.9 %collective-permute-done.5 = bf16[24,4096]{1,0:T(8,128)(2,1)S(1)} collective-permute-done((bf16[24,4096]{1,0:T(8,128)(2,1)S(1)}, bf16[24,4096]{1,0:T(8,128)(2,1)S(1)}, u32[]{:S(2)}, u32[]{:S(2)}) %collective-permute-start.5) | collective-permute-done | bytes 196640 | tf_op jit(solution)/shard_map/ppermute | solution.py:121
  30.3 0.8 %fusion.90 = bf16[48,512]{1,0:T(8,128)(2,1)S(1)} fusion(bf16[48,4096]{1,0:T(8,128)(2,1)S(1)} %collective-permute-done, bf16[1,4096,512]{2,1,0:T(8,128)(2,1)S(1)} %copy-done.1), kind=kOutput, calls=%fused_computation.87 | convolution fusion | flops 201351168 | bytes 4636672 | tf_op jit(solution)/shard_map/dot_general | solution.py:20
  31.3 0.8 %fusion.9 = bf16[48,4096]{1,0:T(8,128)(2,1)S(1)} fusion(bf16[48,512]{1,0:T(8,128)(2,1)S(1)} %bitcast.323, bf16[1,512,4096]{2,1,0:T(8,128)(2,1)S(1)} %copy-done.2, f32[4096]{0:T(1024)S(1)} %bitcast.311), kind=kOutput, calls=%fused_computation.15 | convolution fusion | flops 201719808 | bytes 4653056 | tf_op jit(solution)/shard_map/dot_general | solution.py:36
  32.4 2.0 %collective-permute-start.1 = (bf16[48,4096]{1,0:T(8,128)(2,1)S(1)}, bf16[48,4096]{1,0:T(8,128)(2,1)S(1)}, u32[]{:S(2)}, u32[]{:S(2)}) collective-permute-start(bf16[48,4096]{1,0:T(8,128)(2,1)S(1)} %fusion.9), channel_id=1, source_target_pairs={{0,16},{16,0},{1,17},{17,1},{2,18},{18,2},{3,19},{19,3},{4,20},{20... | collective-permute-start | bytes 1179656 | tf_op jit(solution)/shard_map/ppermute | solution.py:121
  35.1 3.8 %collective-permute-done.2 = bf16[56,4096]{1,0:T(8,128)(2,1)S(1)} collective-permute-done((bf16[56,4096]{1,0:T(8,128)(2,1)S(1)}, bf16[56,4096]{1,0:T(8,128)(2,1)S(1)}, u32[]{:S(2)}, u32[]{:S(2)}) %collective-permute-start.2) | collective-permute-done | bytes 458784 | tf_op jit(solution)/shard_map/ppermute | solution.py:121
  40.2 0.8 %fusion.7 = bf16[56,4096]{1,0:T(8,128)(2,1)S(1)} fusion(bf16[56,512]{1,0:T(8,128)(2,1)S(1)} %bitcast.318, bf16[1,512,4096]{2,1,0:T(8,128)(2,1)S(1)} %copy-done.2, f32[4096]{0:T(1024)S(1)} %bitcast.313), kind=kOutput, calls=%fused_computation.13 | convolution fusion | flops 235339776 | bytes 4726784 | tf_op jit(solution)/shard_map/dot_general | solution.py:36
  41.0 2.0 %collective-permute-start.3 = (bf16[56,4096]{1,0:T(8,128)(2,1)S(1)}, bf16[56,4096]{1,0:T(8,128)(2,1)S(1)}, u32[]{:S(2)}, u32[]{:S(2)}) collective-permute-start(bf16[56,4096]{1,0:T(8,128)(2,1)S(1)} %fusion.7), channel_id=1, source_target_pairs={{0,16},{16,0},{1,17},{17,1},{2,18},{18,2},{3,19},{19,3},{4,20},{20... | collective-permute-start | bytes 1376264 | tf_op jit(solution)/shard_map/ppermute | solution.py:121
  43.0 4.3 %collective-permute-done.1 = bf16[48,4096]{1,0:T(8,128)(2,1)S(1)} collective-permute-done((bf16[48,4096]{1,0:T(8,128)(2,1)S(1)}, bf16[48,4096]{1,0:T(8,128)(2,1)S(1)}, u32[]{:S(2)}, u32[]{:S(2)}) %collective-permute-start.1) | collective-permute-done | bytes 393248 | tf_op jit(solution)/shard_map/ppermute | solution.py:121
  47.7 0.8 %fusion.87 = bf16[48,512]{1,0:T(8,128)(2,1)S(1)} fusion(bf16[48,4096]{1,0:T(8,128)(2,1)S(1)} %fusion.138, bf16[1,4096,512]{2,1,0:T(8,128)(2,1)S(1)} %copy-done.1), kind=kOutput, calls=%fused_computation.86 | convolution fusion | flops 201351168 | bytes 4636672 | tf_op jit(solution)/shard_map/dot_general | solution.py:20
  48.7 0.9 %fusion.140 = bf16[48,4096]{1,0:T(8,128)(2,1)S(1)} fusion(bf16[48,4096]{1,0:T(8,128)(2,1)S(1)} %fusion.138, bf16[48,512]{1,0:T(8,128)(2,1)S(1)} %bitcast.322, bf16[1,512,4096]{2,1,0:T(8,128)(2,1)S(1)} %copy-done.2, f32[4096]{0:T(1024)S(1)} %bitcast.314, pred[]{:T(512)S(6)} %eq.3, bf16[1,1,128,4096]{3,2,1,0:T(8,128)(2,1)S(1)} %copy-done.3), kind=kOutput, calls=%fused_computation.127 | convolution fusion | flops 202702848 | bytes 5439489 | tf_op jit(solution)/shard_map/dot_general | solution.py:36
  49.7 6.5 %collective-permute-done.3 = bf16[56,4096]{1,0:T(8,128)(2,1)S(1)} collective-permute-done((bf16[56,4096]{1,0:T(8,128)(2,1)S(1)}, bf16[56,4096]{1,0:T(8,128)(2,1)S(1)}, u32[]{:S(2)}, u32[]{:S(2)}) %collective-permute-start.3) | collective-permute-done | bytes 458784 | tf_op jit(solution)/shard_map/ppermute | solution.py:121
  56.6 0.8 %fusion.75 = bf16[56,512]{1,0:T(8,128)(2,1)S(1)} fusion(bf16[56,4096]{1,0:T(8,128)(2,1)S(1)} %fusion.136, bf16[1,4096,512]{2,1,0:T(8,128)(2,1)S(1)} %copy-done.1), kind=kOutput, calls=%fused_computation.80 | convolution fusion | flops 234909696 | bytes 4710400 | tf_op jit(solution)/shard_map/dot_general | solution.py:20
  57.7 1.0 %fusion.139 = bf16[56,4096]{1,0:T(8,128)(2,1)S(1)} fusion(bf16[56,4096]{1,0:T(8,128)(2,1)S(1)} %fusion.136, bf16[56,512]{1,0:T(8,128)(2,1)S(1)} %bitcast.317, bf16[1,512,4096]{2,1,0:T(8,128)(2,1)S(1)} %copy-done.2, f32[4096]{0:T(1024)S(1)} %bitcast.315, pred[]{:T(512)S(6)} %eq.3, bf16[1,1,128,4096]{3,2,1,0:T(8,128)(2,1)S(1)} %copy-done.3), kind=kOutput, calls=%fused_computation.126 | convolution fusion | flops 236486656 | bytes 5644289 | tf_op jit(solution)/shard_map/dot_general | solution.py:36
  58.7 1.0 %maximum_bitcast_fusion = bf16[1,1,128,4096]{3,2,1,0:T(8,128)(2,1)} fusion(bf16[24,4096]{1,0:T(8,128)(2,1)S(1)} %fusion.153, bf16[56,4096]{1,0:T(8,128)(2,1)S(1)} %fusion.139, bf16[48,4096]{1,0:T(8,128)(2,1)S(1)} %fusion.140), kind=kLoop, calls=%fused_computation.119 | loop fusion | flops 3145728 | bytes 2097152 | tf_op jit(solution)/shard_map/reshape | solution.py:147
  (67 shorter events, 7.9 us)
Async XLA Ops:
  0.0 4.3 %copy-start = (bf16[1,2,256,256]{3,2,1,0:T(8,128)(2,1)S(1)}, bf16[1,2,256,256]{3,2,1,0:T(8,128)(2,1)}, u32[]{:S(2)}) copy-start(bf16[1,2,256,256]{3,2,1,0:T(8,128)(2,1)} %param.8) | copy-start | bytes 786436
  0.0 4.5 %copy-start.3 = (bf16[1,1,128,4096]{3,2,1,0:T(8,128)(2,1)S(1)}, bf16[1,1,128,4096]{3,2,1,0:T(8,128)(2,1)}, u32[]{:S(2)}) copy-start(bf16[1,1,128,4096]{3,2,1,0:T(8,128)(2,1)} %param.6) | copy-start | bytes 3145732
  0.0 4.5 %copy-start.4 = (f32[1,4096]{1,0:T(1,128)S(1)}, f32[1,4096]{1,0:T(1,128)}, u32[]{:S(2)}) copy-start(f32[1,4096]{1,0:T(1,128)} %param.11) | copy-start | bytes 49156
  1.3 9.3 %copy-start.5 = (bf16[1,2,4096]{2,1,0:T(2,128)(2,1)S(1)}, bf16[1,2,4096]{2,1,0:T(2,128)(2,1)}, u32[]{:S(2)}) copy-start(bf16[1,2,4096]{2,1,0:T(2,128)(2,1)} %param.10) | copy-start | bytes 49156
  4.5 6.3 %copy-start.1 = (bf16[1,4096,512]{2,1,0:T(8,128)(2,1)S(1)}, bf16[1,4096,512]{2,1,0:T(8,128)(2,1)}, u32[]{:S(2)}) copy-start(bf16[1,4096,512]{2,1,0:T(8,128)(2,1)} %param.7) | copy-start | bytes 12582916
  4.5 7.4 %copy-start.2 = (bf16[1,512,4096]{2,1,0:T(8,128)(2,1)S(1)}, bf16[1,512,4096]{2,1,0:T(8,128)(2,1)}, u32[]{:S(2)}) copy-start(bf16[1,512,4096]{2,1,0:T(8,128)(2,1)} %param.9) | copy-start | bytes 12582916
  7.5 8.4 %collective-permute-start.4 = (bf16[24,4096]{1,0:T(8,128)(2,1)S(1)}, bf16[24,4096]{1,0:T(8,128)(2,1)S(1)}, u32[]{:S(2)}, u32[]{:S(2)}) collective-permute-start(bf16[24,4096]{1,0:T(8,128)(2,1)S(1)} %fusion.17), channel_id=1, source_target_pairs={{0,16},{16,0},{1,17},{17,1},{2,18},{18,2},{3,19},{19,3},{4,20},{20... | collective-permute-start | bytes 589832 | tf_op jit(solution)/shard_map/ppermute | solution.py:121
  12.8 17.3 %collective-permute-start = (bf16[48,4096]{1,0:T(8,128)(2,1)S(1)}, bf16[48,4096]{1,0:T(8,128)(2,1)S(1)}, u32[]{:S(2)}, u32[]{:S(2)}) collective-permute-start(bf16[48,4096]{1,0:T(8,128)(2,1)S(1)} %fusion.11), channel_id=1, source_target_pairs={{0,16},{16,0},{1,17},{17,1},{2,18},{18,2},{3,19},{19,3},{4,20},{20... | collective-permute-start | bytes 1179656 | tf_op jit(solution)/shard_map/ppermute | solution.py:121
  17.7 11.4 %collective-permute-start.5 = (bf16[24,4096]{1,0:T(8,128)(2,1)S(1)}, bf16[24,4096]{1,0:T(8,128)(2,1)S(1)}, u32[]{:S(2)}, u32[]{:S(2)}) collective-permute-start(bf16[24,4096]{1,0:T(8,128)(2,1)S(1)} %fusion.16), channel_id=1, source_target_pairs={{0,16},{16,0},{1,17},{17,1},{2,18},{18,2},{3,19},{19,3},{4,20},{20... | collective-permute-start | bytes 589832 | tf_op jit(solution)/shard_map/ppermute | solution.py:121
  21.0 17.8 %collective-permute-start.2 = (bf16[56,4096]{1,0:T(8,128)(2,1)S(1)}, bf16[56,4096]{1,0:T(8,128)(2,1)S(1)}, u32[]{:S(2)}, u32[]{:S(2)}) collective-permute-start(bf16[56,4096]{1,0:T(8,128)(2,1)S(1)} %fusion.10), channel_id=1, source_target_pairs={{0,16},{16,0},{1,17},{17,1},{2,18},{18,2},{3,19},{19,3},{4,20},{20... | collective-permute-start | bytes 1376264 | tf_op jit(solution)/shard_map/ppermute | solution.py:121
  32.4 14.9 %collective-permute-start.1 = (bf16[48,4096]{1,0:T(8,128)(2,1)S(1)}, bf16[48,4096]{1,0:T(8,128)(2,1)S(1)}, u32[]{:S(2)}, u32[]{:S(2)}) collective-permute-start(bf16[48,4096]{1,0:T(8,128)(2,1)S(1)} %fusion.9), channel_id=1, source_target_pairs={{0,16},{16,0},{1,17},{17,1},{2,18},{18,2},{3,19},{19,3},{4,20},{20... | collective-permute-start | bytes 1179656 | tf_op jit(solution)/shard_map/ppermute | solution.py:121
  41.0 15.2 %collective-permute-start.3 = (bf16[56,4096]{1,0:T(8,128)(2,1)S(1)}, bf16[56,4096]{1,0:T(8,128)(2,1)S(1)}, u32[]{:S(2)}, u32[]{:S(2)}) collective-permute-start(bf16[56,4096]{1,0:T(8,128)(2,1)S(1)} %fusion.7), channel_id=1, source_target_pairs={{0,16},{16,0},{1,17},{17,1},{2,18},{18,2},{3,19},{19,3},{4,20},{20... | collective-permute-start | bytes 1376264 | tf_op jit(solution)/shard_map/ppermute | solution.py:121
